TPU v7x, 32 devices: a whole 2x2x4 slice. The times are simulated.
32 devices in a mesh: owner: 4 (over y, core), rows: 8 (over z, x).
Axes of the slice: x: 2, y: 2, z: 4, core: 2. Of those that a mesh axis runs over, the one named last changes fastest.
Arguments:
- w_down: float32 [16, 6400, 4096], P('owner', None, 'rows'), may hold values from -0.109375 to 0.109375
- avg_down: bfloat16 [16, 6400, 4096], P('owner', None, 'rows'), may hold values from -0.0390625 to 0.0390625
- router_weight: float32 [4096, 16], P('rows', 'owner'), may hold values from -0.09375 to 0.09375
- router_gain: float32 [4096], P('rows'), may hold values from 0.25 to 1.75
Outputs:
- serve_down: bfloat16 [16, 6400, 4096], P('owner', 'rows')
- scale_down: float32 [16, 6400], P('owner', 'rows')
- serve_router: bfloat16 [4096, 16], replicated
All inputs are finite; a program needn't handle non-finite values.
Results may differ from a plain program's by a relative error of at most 0.0085.
Values may be sent and summed in bfloat16 or wider, within the bound.
A program may use at most 256 MiB of HBM per device.

v0:
```python
import jax
import jax.numpy as jnp
from jax import lax
from jax.sharding import PartitionSpec as P


def local(w_down, avg_down, router_weight, router_gain):
    fresh_down = w_down + avg_down.astype(jnp.float32)
    total_down = lax.psum(
        jnp.sum(fresh_down * fresh_down, axis=2).astype(jnp.bfloat16), "rows"
    ).astype(jnp.float32)
    scale_down = jnp.sqrt(total_down)
    narrow_down = (fresh_down / jnp.expand_dims(scale_down, 2)).astype(jnp.bfloat16)
    serve_down = lax.all_to_all(narrow_down, "rows", split_axis=1, concat_axis=2, tiled=True)
    scale_down = lax.dynamic_slice_in_dim(
        scale_down, lax.axis_index("rows") * serve_down.shape[1], serve_down.shape[1], axis=1
    )
    part_router = (router_weight * router_gain[:, None]).astype(jnp.bfloat16)
    row_router = lax.all_gather(part_router, "rows", axis=0, tiled=True)
    serve_router = lax.all_gather(row_router, "owner", axis=1, tiled=True)
    return (serve_down, scale_down, serve_router)


def solution(mesh):
    return jax.shard_map(
        local,
        mesh=mesh,
        in_specs=(
            P("owner", None, "rows"),
            P("owner", None, "rows"),
            P("rows", "owner"),
            P("rows"),
        ),
        out_specs=(P("owner", "rows", None), P("owner", "rows"), P()),
        check_vma=False,
    )
```

profile of v0, /device:TPU:0, one launch (start us, length us, event | category | flops | bytes accessed | tf_op | source)
XLA Modules:
  0.0 826.9 jit_solution(7862156734528137198)
XLA Ops:
  0.6 24.2 %multiply_reduce_fusion = bf16[4,6400]{1,0:T(4,128)(2,1)S(1)} fusion(f32[4,6400,512]{2,1,0:T(8,128)} %param.4, bf16[4,6400,512]{2,1,0:T(8,128)(2,1)} %param.5), kind=kLoop, calls=%fused_computation.1 | loop fusion | flops 52403200 | bytes 78694400 | tf_op jit(solution)/shard_map/reduce_sum | solution.py:10
  24.9 0.9 copy.21
  25.8 83.5 %psum.7 = bf16[4,6400]{0,1:T(8,128)(2,1)} all-reduce(bf16[4,6400]{0,1:T(8,128)(2,1)S(1)} %copy.21), channel_id=1, replica_groups=mesh['owner'=4,'rows'=8] {'rows'}, use_global_device_ids=true, to_apply=%region_1.0 | all-reduce | flops 25600 | bytes 102400 | tf_op jit(solution)/shard_map/psum | solution.py:9
  109.3 2.3 convert_sqrt_fusion
  111.6 1.2 copy.17
  112.8 34.3 %divide_convert_fusion = bf16[4,6400,512]{2,1,0:T(8,128)(2,1)} fusion(f32[4,6400,512]{2,1,0:T(8,128)} %param.4, bf16[4,6400,512]{2,1,0:T(8,128)(2,1)} %param.5, f32[4,6400]{1,0:T(4,128)S(1)} %copy.17), kind=kLoop, calls=%fused_computation | loop fusion | flops 52428800 | bytes 104960000 | tf_op jit(solution)/shard_map/convert_element_type | solution.py:13
  147.1 33.4 %copy.18 = bf16[4,6400,512]{2,0,1:T(4,128)(2,1)} copy(bf16[4,6400,512]{2,1,0:T(8,128)(2,1)} %divide_convert_fusion) | data formatting | bytes 52428800 | tf_op jit(solution)/shard_map/convert_element_type | solution.py:13
  180.5 0.0 copy-start
  180.5 0.0 copy-start.1
  180.5 6.6 all-to-all-start
  187.2 0.8 constant_dynamic-slice_fusion
  187.9 1.8 copy.20
  189.7 0.0 copy-done
  189.7 0.0 copy-done.1
  189.7 573.7 %all_gather.6 = bf16[4096,4]{0,1:T(4,128)(2,1)S(1)} all-gather(bf16[512,4]{0,1:T(4,128)(2,1)S(1)} %multiply_convert_fusion), channel_id=1, replica_groups=mesh['owner'=4,'rows'=8] {'rows'}, dimensions={0}, use_global_device_ids=true | all-gather | bytes 36864 | tf_op jit(solution)/shard_map/all_gather | solution.py:19
  763.4 5.4 all-gather
  768.8 0.7 reshape.9
  769.5 0.0 all-to-all-done
  769.5 18.2 %copy.19 = bf16[4,800,8,512]{3,2,1,0:T(8,128)(2,1)} copy(bf16[4,800,8,512]{3,0,1,2:T(4,128)(2,1)} %bitcast.1) | data formatting | bytes 52428800 | tf_op jit(solution)/shard_map/all_to_all | solution.py:14
  787.7 39.2 %all_to_all.16 = bf16[4,800,4096]{2,1,0:T(8,128)(2,1)} reshape(bf16[4,800,8,512]{3,2,1,0:T(8,128)(2,1)} %copy.19) | data formatting | bytes 52428800 | tf_op jit(solution)/shard_map/all_to_all | solution.py:14
  (1 shorter events, 0.0 us)
Async XLA Ops:
  180.5 9.2 %copy-start = (f32[512,4]{0,1:T(4,128)S(1)}, f32[512,4]{0,1:T(4,128)}, u32[]{:S(2)}) copy-start(f32[512,4]{0,1:T(4,128)} %param.6) | copy-start | bytes 24580
  180.5 9.2 %copy-start.1 = (f32[512]{0:T(512)S(1)}, f32[512]{0:T(512)}, u32[]{:S(2)}) copy-start(f32[512]{0:T(512)} %param.7) | copy-start | bytes 6148
  180.5 589.0 %all-to-all-start = ((bf16[4,6400,512]{2,0,1:T(4,128)(2,1)}), bf16[4,6400,512]{2,0,1:T(4,128)(2,1)}, u32[]{:S(2)}, u32[]{:S(2)}) async-start(bf16[4,6400,512]{2,0,1:T(4,128)(2,1)} %copy.18), calls=%async_computation | async-start | bytes 52428800 | tf_op jit(solution)/shard_map/all_to_all | solution.py:14
where the time goes:
time: 828 us; the launch traced here: 827 us
  blocking collectives  663 us (80%)
  local copies, waits for them, and re-layouts  96.2 us (12%)
  other arithmetic  60.8 us (7%)
    all_gather x1, blocking collectives, local(): row_router = lax.all_gather(part_router, 'rows', axis=0, tiled=True)  574 us
    psum x1, blocking collectives, local(): lax.psum(jnp.sum(fresh_down * fresh_down, axis=2).astype(jnp.bfloat16), '...  83.5 us
    all_to_all x2, local copies, waits for them, and re-layouts, local(): lax.all_to_all(narrow_down, 'rows', split_axis=1, concat_axis=2, tiled=True)  57.4 us
    convert_element_type x1, other arithmetic, local(): (fresh_down / jnp.expand_dims(scale_down, 2)).astype(jnp.bfloat16)  34.3 us
    convert_element_type x1, local copies, waits for them, and re-layouts, local(): (fresh_down / jnp.expand_dims(scale_down, 2)).astype(jnp.bfloat16)  33.4 us
    reduce_sum x1, other arithmetic, local(): jnp.sum(fresh_down * fresh_down, axis=2).astype(jnp.bfloat16)  24.2 us
  transfers between devices with their start and end apart: 1, of which 0 were waited for; matrix products, arithmetic and copies ran while one was open for 0% of the time, Pallas kernels for 0%

commit v1 on v0

v1 whole, which is shorter than its diff:
```python
import functools
import math

import jax
import jax.numpy as jnp
from jax import lax
from jax.experimental import pallas as pl
from jax.experimental.pallas import tpu as pltpu
from jax.sharding import PartitionSpec as P

MESH = pl.DeviceIdType.MESH
ANY = pl.ANY
TAIL_SHARE = 13


def divisor(size, most, step):
    for d in range(min(size, most) // step * step, 0, -step):
        if size % d == 0:
            return d
    return size


def receiver(n, me, t):
    if n % 4:
        return lax.rem(me + 1 + t, n)
    half = n // 2
    side, place = me // half, lax.rem(me, half)
    middle = lax.rem((me + n // 4) // half, 2)
    u = lax.rem(t + (1 - middle) * half, n - 1)
    across = u // half
    i = u - across * (half - 1)
    to_side = (1 - side) * (1 - across) + side * across
    return to_side * half + lax.rem(place + i, half)


def exchange_body(n, keep, w, a, r, got, tail, gotr, wbuf, abuf, packed, in_sem, send_sem, recv_sem, own_sem, tail_sem, r_sem):
    experts, _, per, cols = w.shape
    me = lax.axis_index("rows")
    block = divisor(per, 80, 8)
    rows_of = [per] * (experts - 1) + [per - keep]

    def dest(t):
        return jnp.where(t == n - 1, me, receiver(n, me, jnp.minimum(t, n - 2)))

    def loads(t, e):
        d = dest(t)
        return (
            pltpu.make_async_copy(w.at[e, d], wbuf.at[e], in_sem.at[0, e]),
            pltpu.make_async_copy(a.at[e, d], abuf.at[e], in_sem.at[1, e]),
        )

    def remote(src_dev, to, e):
        rows = pl.ds(e * per, rows_of[e])
        return pltpu.make_async_remote_copy(
            src_ref=packed.at[to, rows],
            dst_ref=got.at[src_dev, rows],
            send_sem=send_sem.at[to, e],
            recv_sem=recv_sem.at[src_dev, e],
            device_id={"rows": to},
            device_id_type=MESH,
        )

    def own(e):
        rows = pl.ds(e * per, rows_of[e])
        return pltpu.make_async_copy(packed.at[me, rows], got.at[me, rows], own_sem.at[e])

    def tail_copy(d):
        rows = pl.ds(experts * per - keep, keep)
        return pltpu.make_async_copy(packed.at[d, rows], tail.at[d], tail_sem.at[d])

    def r_remote(src_dev, to):
        return pltpu.make_async_remote_copy(
            src_ref=r,
            dst_ref=gotr.at[src_dev],
            send_sem=r_sem.at[0, to],
            recv_sem=r_sem.at[1, src_dev],
            device_id={"rows": to},
            device_id_type=MESH,
        )

    def r_own():
        return pltpu.make_async_copy(r, gotr.at[me], r_sem.at[0, me])

    for e in range(experts):
        for copy in loads(0, e):
            copy.start()
    barrier = pltpu.get_barrier_semaphore()

    @pl.loop(1, n)
    def _(i):
        pl.semaphore_signal(barrier, inc=1, device_id={"rows": lax.rem(me + i, n)}, device_id_type=MESH)

    pl.semaphore_wait(barrier, n - 1)
    r_own().start()

    def send(t, e):
        @pl.when(t < n - 1)
        def _():
            remote(me, dest(t), e).start()

        @pl.when(t == n - 1)
        def _():
            own(e).start()

        if e == experts - 1:
            tail_copy(dest(t)).start()

    @pl.loop(0, n)
    def _(t):
        d = dest(t)
        for e in range(experts):
            for copy in loads(t, e):
                copy.wait()
            if e:
                send(t, e - 1)
            else:

                @pl.when(t > 0)
                def _():
                    send(t - 1, experts - 1)

            @pl.loop(0, per // block)
            def _(b):
                rows = pl.ds(pl.multiple_of(b * block, block), block)
                into = pl.ds(pl.multiple_of(e * per + b * block, math.gcd(block, per)), block)
                packed[d, into] = (wbuf[e, rows] + abuf[e, rows].astype(jnp.float32)).astype(packed.dtype)

            @pl.when(t < n - 1)
            def _():
                for copy in loads(t + 1, e):
                    copy.start()

    send(n - 1, experts - 1)

    @pl.loop(1, n)
    def _(i):
        r_remote(me, lax.rem(me + i, n)).start()

    @pl.loop(1, n)
    def _(i):
        other = lax.rem(me + i, n)
        for e in range(experts):
            remote(me, other, e).wait_send()
            remote(other, me, e).wait_recv()
        r_remote(me, other).wait_send()
        r_remote(other, me).wait_recv()
        tail_copy(other).wait()

    for e in range(experts):
        own(e).wait()
    tail_copy(me).wait()
    r_own().wait()


def exchange(n, keep, w, a, r):
    experts, _, per, cols = w.shape
    any_spec = pl.BlockSpec(memory_space=ANY)
    bf16 = jnp.bfloat16
    return pl.pallas_call(
        functools.partial(exchange_body, n, keep),
        in_specs=[any_spec] * 3,
        out_specs=[any_spec] * 3,
        out_shape=[
            jax.ShapeDtypeStruct((n, experts * per - keep, cols), bf16),
            jax.ShapeDtypeStruct((n, keep, cols), bf16),
            jax.ShapeDtypeStruct((n,) + r.shape, bf16),
        ],
        scratch_shapes=[
            pltpu.VMEM((experts, per, cols), jnp.float32),
            pltpu.VMEM((experts, per, cols), bf16),
            pltpu.VMEM((n, experts * per, cols), bf16),
            pltpu.SemaphoreType.DMA((2, experts)),
            pltpu.SemaphoreType.DMA((n, experts)),
            pltpu.SemaphoreType.DMA((n, experts)),
            pltpu.SemaphoreType.DMA((experts,)),
            pltpu.SemaphoreType.DMA((n,)),
            pltpu.SemaphoreType.DMA((2, n)),
        ],
        compiler_params=pltpu.CompilerParams(
            collective_id=0, has_side_effects=True, vmem_limit_bytes=63 * 2**20
        ),
        name="exchange",
    )(w, a, r)


def norm_body(n, cols, got, *rest):
    serve, scale = rest[-2:]
    total = None
    for s in range(n):
        x = got[s].astype(jnp.float32)
        part = jnp.sum(x * x, axis=1, keepdims=True)
        total = part if total is None else total + part
    root = jnp.sqrt(total)
    inverse = 1.0 / root
    for s in range(n):
        x = got[s].astype(jnp.float32)
        serve[:, s * cols : (s + 1) * cols] = (x * inverse).astype(serve.dtype)
    scale[...] = jnp.broadcast_to(root, scale.shape)


def norm(got, serve, first, count, rb):
    n, here, cols = got.shape
    specs, args, alias = [pl.BlockSpec((n, rb, cols), lambda i: (0, i, 0))], [got], {}
    if serve is not None:
        specs.append(pl.BlockSpec(memory_space=ANY))
        args.append(serve)
        alias = {1: 0}
    return pl.pallas_call(
        functools.partial(norm_body, n, cols),
        grid=(here // rb,),
        in_specs=specs,
        out_specs=[
            pl.BlockSpec((rb, n * cols), lambda i: (first // rb + i, 0)),
            pl.BlockSpec((rb, 128), lambda i: (i, 0)),
        ],
        out_shape=[
            jax.ShapeDtypeStruct((count, n * cols), jnp.bfloat16),
            jax.ShapeDtypeStruct((here, 128), jnp.float32),
        ],
        input_output_aliases=alias,
        cost_estimate=pl.CostEstimate(
            flops=6 * n * here * cols, bytes_accessed=4 * n * here * cols, transcendentals=0
        ),
        name="norm",
    )(*args)


def local(n, w_down, avg_down, router_weight, router_gain):
    experts, rows, cols = w_down.shape
    per = rows // n
    mine = router_weight.shape[1]
    keep = per % 16 + 16 * max(1, -(-experts * per // TAIL_SHARE) // 16)
    keep = min(keep, per)
    count = experts * per
    rb = divisor(math.gcd(count - keep, keep), 80, 8)
    part = (router_weight * router_gain[:, None]).astype(jnp.bfloat16).T
    part = jnp.pad(part, ((0, -mine % 16), (0, 0)))
    got, tail, gotr = exchange(
        n, keep, w_down.reshape(experts, n, per, cols), avg_down.reshape(experts, n, per, cols), part
    )
    last = lax.all_to_all(tail, "rows", split_axis=0, concat_axis=0, tiled=True)
    rows_of = gotr[:, :mine, :].transpose(1, 0, 2).reshape(mine, n * cols)
    router = lax.all_gather(rows_of, "owner", axis=0, tiled=True).T
    serve, scale = norm(got, None, 0, count, rb)
    scale = scale[:, 0]
    serve, scale, last, router = lax.optimization_barrier((serve, scale, last, router))
    serve, scale_last = norm(last, serve, count - keep, count, rb)
    scale = jnp.concatenate([scale, scale_last[:, 0]]).reshape(experts, per)
    return serve.reshape(experts, per, n * cols), scale, router


def solution(mesh):
    return jax.shard_map(
        functools.partial(local, mesh.shape["rows"]),
        mesh=mesh,
        in_specs=(
            P("owner", None, "rows"),
            P("owner", None, "rows"),
            P("rows", "owner"),
            P("rows"),
        ),
        out_specs=(P("owner", "rows", None), P("owner", "rows"), P()),
        check_vma=False,
    )
```

time: 828 us -> 590 us (0.71)
  blocking collectives: 663 us -> 5.42 us
  Pallas kernels: 0 us -> 568 us
  local copies, waits for them, and re-layouts: 96.2 us -> 6.99 us
  other arithmetic: 60.8 us -> 0.78 us
    all_gather x2 -> x1, blocking collectives: 579 us -> 5.42 us  [local(): router = lax.all_gather(rows_of, 'owner', axis=0, tiled=True).T]
    pallas_call x0 -> x3, Pallas kernels: none -> 568 us  [the longest x1 531 us: exchange(): pl.pallas_call(functools.partial(exchange_body, n, keep), in_specs=[any_s...]
    psum x1 -> x0, blocking collectives: 83.5 us -> none  [local(): lax.psum(jnp.sum(fresh_down * fresh_down, axis=2).astype(jnp.bfloat16), '...]
    all_to_all x2 -> x0, local copies, waits for them, and re-layouts: 57.4 us -> none  [local(): lax.all_to_all(narrow_down, 'rows', split_axis=1, concat_axis=2, tiled=True)]
    convert_element_type x2 -> x0, other arithmetic: 34.3 us -> none  [the longest x1 34.3 us: local(): (fresh_down / jnp.expand_dims(scale_down, 2)).astype(jnp.bfloat16)]
    convert_element_type x1 -> x0, local copies, waits for them, and re-layouts: 33.4 us -> none  [local(): (fresh_down / jnp.expand_dims(scale_down, 2)).astype(jnp.bfloat16)]
    reduce_sum x1 -> x0, other arithmetic: 24.2 us -> none  [local(): jnp.sum(fresh_down * fresh_down, axis=2).astype(jnp.bfloat16)]
  transfers between devices with their start and end apart: 1 -> 1, of which waited for: 0 -> 1; matrix products, arithmetic and copies ran while one was open for 0% -> 1% of each run, Pallas kernels for 0% -> 6%
where the time goes in v1:
time: 590 us; the launch traced here: 589 us
  Pallas kernels  568 us (96%)
  local copies, waits for them, and re-layouts  6.99 us (1%)
    pallas_call x1, Pallas kernels, exchange(): pl.pallas_call(functools.partial(exchange_body, n, keep), in_specs=[any_s...  531 us
    pallas_call x2, Pallas kernels, norm(): pl.pallas_call(functools.partial(norm_body, n, cols), grid=(here // rb,),...  37.2 us
  transfers between devices with their start and end apart: 1, of which 1 were waited for; matrix products, arithmetic and copies ran while one was open for 1% of the time, Pallas kernels for 6%

profile of v1, /device:TPU:0, one launch (start us, length us, event | category | flops | bytes accessed | tf_op | source)
XLA Modules:
  0.0 588.8 jit_solution(17346900091774144757)
XLA Ops:
  0.6 0.7 fusion
  1.3 0.6 pad.4.r
  1.9 531.2 %exchange.1 = (bf16[8,2960,512]{2,1,0:T(8,128)(2,1)}, bf16[8,240,512]{2,1,0:T(8,128)(2,1)}, bf16[8,16,512]{2,1,0:T(8,128)(2,1)}) custom-call(f32[4,8,800,512]{3,2,1,0:T(8,128)} %bitcast.9, bf16[4,8,800,512]{3,2,1,0:T(8,128)(2,1)} %bitcast.11, bf16[16,512]{1,0:T(8,128)(2,1)} %pad.4.r), custom_call_target="tpu_custom_call" | custom-call | tf_op jit(solution)/shard_map/exchange/pallas_call | solution.py:159
  533.1 4.2 all-to-all-start
  537.3 0.8 slice.10
  538.2 5.4 all-gather
  543.6 0.7 reshape.28
  544.3 33.1 %norm.2 = (bf16[3200,4096]{1,0:T(8,128)(2,1)}, f32[2960,128]{1,0:T(8,128)}) custom-call(bf16[8,2960,512]{2,1,0:T(8,128)(2,1)} %get-tuple-element.14.got), custom_call_target="tpu_custom_call" | custom-call | flops 72744960 | bytes 48496640 | tf_op jit(solution)/shard_map/norm/pallas_call | solution.py:208
  577.3 1.9 slice_reduce_fusion
  579.2 2.4 all-to-all-done.got
  581.6 0.0 copy-start
  581.6 1.3 copy-done
  582.9 4.1 norm.3
  587.0 1.0 slice_reduce_fusion.1
  588.0 0.1 pad_maximum_fusion
  588.1 0.7 reshape.26
Async XLA Ops:
  533.1 48.5 %all-to-all-start = ((bf16[8,240,512]{2,1,0:T(8,128)(2,1)}), bf16[8,240,512]{2,1,0:T(8,128)(2,1)S(1)}, u32[]{:S(2)}, u32[]{:S(2)}) async-start(bf16[8,240,512]{2,1,0:T(8,128)(2,1)} %get-tuple-element.17), calls=%async_computation | async-start | bytes 3932160 | tf_op jit(solution)/shard_map/all_to_all | solution.py:241
  581.6 1.3 copy-start
